TPU v7x, 32 devices: a whole 2x2x4 slice. The times are simulated.
32 devices in a mesh: rep: 8 (over y, x, core), grp: 4 (over z).
Axes of the slice: x: 2, y: 2, z: 4, core: 2. Of those that a mesh axis runs over, the one named last changes fastest.
Arguments:
- frames: bfloat16 [8192, 768], P(('rep', 'grp')), may hold values from -6 to 6
- cotangent: bfloat16 [8192, 768], P(('rep', 'grp')), may hold values from -6 to 6
- params: bfloat16 [4, 1771776], P('grp'), may hold values from -8 to 8, as said below
- first_moment: float32 [4, 1771776], P('grp'), as said below
- second_moment: float32 [4, 1771776], P('grp'), as said below
Outputs:
- out_frames: bfloat16 [8192, 768], P(('rep', 'grp'))
- frames_grad: bfloat16 [8192, 768], P(('rep', 'grp'))
- param_grad: float32 [4, 1771776], P('grp')
- new_params: float32 [4, 1771776], P('grp')
- new_first: float32 [4, 1771776], P('grp')
- new_second: float32 [4, 1771776], P('grp')
Inputs may be any that keep to these rules, and one draw needn't show every extreme that they name: `params`: laid out as the first step says; gains lie between 0.5 and 1.5. `first_moment`: laid out as the first step says. `second_moment`: Positive; laid out as the first step says.
All inputs are finite; a program needn't handle non-finite values.
Results may differ from a plain program's by a relative error of at most 0.012.
The roundings to bfloat16 on the way count: a program that leaves them out, or rounds other values in their place, can miss the bound.
Values may be sent and summed in bfloat16 or wider, within the bound.
A program may use at most 256 MiB of HBM per device.

v0:
```python
import functools
import types

import jax
import jax.numpy as jnp
from jax import lax
from jax.sharding import PartitionSpec as P
from jax.experimental import pallas as pl
from jax.experimental.pallas import tpu as pltpu

MESH = pl.DeviceIdType.MESH
BF = jnp.bfloat16
F32 = jnp.float32
D = 768
FF = 3072
HDIM = 64
LANE = 128
FLAT = 1771776
FROWS = FLAT // LANE


class Mat:
    def __init__(self, offset, block, cols, suba, subb):
        self.offset, self.block, self.cols = offset, block, cols
        self.tiles = cols // LANE
        self.row0 = offset // LANE
        self.shifted = offset % LANE != 0
        self.quarter = block // 4
        self.half = cols // 2
        self.sub = (suba, subb)


QKV = Mat(384, 192, 2304, (0, 48, 0, 640), (0, 48, 640, 512))
OUT = Mat(443136, 192, 768, (0, 48, 0, 128), (0, 48, 128, 256))
UP = Mat(591168, 192, 3072, (0, 48, 0, 768), (0, 48, 768, 768))
DOWN = Mat(1181760, 768, 768, (0, 96, 0, 384), (96, 96, 0, 384))
MATS = (QKV, OUT, UP, DOWN)
SMALL = ((0, 3), (3459, 3), (4614, 5), (9226, 7), (13840, 2))
SROWS = 24


def flip(index, bit):
    return index + bit - 2 * bit * ((index // bit) % 2)


def mo(value, by):
    return pl.multiple_of(value, by)


def part(ref, m, r, k, h, sub=None):
    r0, rn, c0, cn = m.sub[sub] if sub is not None else (0, m.quarter, 0, m.half)
    row = mo(r * m.block + k * m.quarter + r0, 16)
    col = mo(h * m.half + c0, LANE)
    return ref.at[pl.ds(row, rn), pl.ds(col, cn)]


def slab(ref, m, r, h):
    return ref.at[pl.ds(mo(r * m.block, 16), m.block), pl.ds(mo(h * m.half, LANE), m.half)]


def remote(src, dst, send, recv, rep, grp):
    return pltpu.make_async_remote_copy(
        src_ref=src, dst_ref=dst, send_sem=send, recv_sem=recv,
        device_id={"rep": rep, "grp": grp}, device_id_type=MESH)


def greet(rep, g, groups):
    barrier = pltpu.get_barrier_semaphore()
    peers = [(flip(rep, b), g) for b in (1, 2, 4)]
    peers += [(rep, lax.rem(g + i, groups)) for i in range(1, groups)]
    return barrier, peers


def do_barrier(barrier, peers):
    for r, gg in peers:
        pl.semaphore_signal(barrier, inc=1, device_id={"rep": r, "grp": gg}, device_id_type=MESH)
    pl.semaphore_wait(barrier, len(peers))


def add_rows(dst, a, b, rows, step=16):
    def body(i, c):
        at = pl.ds(mo(i * step, 16), step)
        dst[at, :] = (a[at, :].astype(F32) + b[at, :].astype(F32)).astype(dst.dtype)
        return c
    lax.fori_loop(0, rows // step, body, 0)


EPS_NORM = 1e-05
ROOT_HALF = 0.7071067811865476
ROOT_TWO_PI = 0.3989422804014327
HEADS = D // HDIM
GAIN_ONE, SHIFT_ONE, QV_BIAS, OUT_BIAS, GAIN_TWO, SHIFT_TWO, UP_BIAS, DOWN_BIAS = (
    (0, 3), (3, 3), (6, 6), (12, 3), (15, 3), (18, 3), (23, 12), (37, 3))


def low_lanes():
    return lax.broadcasted_iota(jnp.int32, (1, LANE), 1) < 64


def assemble(sm, place, out):
    first, count = place
    halves = [(gi, first + i) for gi in range(sm.shape[0]) for i in range(count)]
    for t in range(len(halves) // 2):
        (g0, h0), (g1, h1) = halves[2 * t], halves[2 * t + 1]
        a = sm[g0, h0 // 2:h0 // 2 + 1, :]
        b = sm[g1, h1 // 2:h1 // 2 + 1, :]
        a = pltpu.roll(a, 64, 1) if h0 % 2 else a
        b = b if h1 % 2 else pltpu.roll(b, 64, 1)
        out[0:1, t * LANE:(t + 1) * LANE] = jnp.where(low_lanes(), a, b)


def fill_image(image, rows, vectors):
    where = {}
    for place, ref in vectors:
        for i in range(place[1]):
            where[place[0] + i] = (place[1], i, ref)
    for gi in range(image.shape[0]):
        for r in rows:
            parts = []
            for side in range(2):
                spot = where.get(2 * r + side)
                if spot is None:
                    parts.append(jnp.zeros((1, LANE), F32))
                    continue
                count, i, ref = spot
                q = gi * count + i
                v = ref[0:1, q // 2 * LANE:(q // 2 + 1) * LANE]
                parts.append(v if q % 2 == side else pltpu.roll(v, 64, 1))
            image[gi, r:r + 1, :] = jnp.where(low_lanes(), parts[0], parts[1])


def mean(v):
    return jnp.sum(v, axis=-1, keepdims=True) * (1.0 / D)


def normalize(v):
    centered = v - mean(v)
    inverse = lax.rsqrt(mean(centered * centered) + EPS_NORM)
    return centered * inverse, inverse


def norm_back(upstream, normal, inverse, gain):
    s = upstream * gain
    return inverse * (s - mean(s) - normal * mean(s * normal))


def nn(a, b):
    return lax.dot_general(a, b, (((1,), (0,)), ((), ())), preferred_element_type=F32)


def nt(a, b):
    return lax.dot_general(a, b, (((1,), (1,)), ((), ())), preferred_element_type=F32)


def loop(count, body):
    def step(i, c):
        body(i)
        return c
    lax.fori_loop(0, count, step, 0)


def head_mask(rows):
    return lax.broadcasted_iota(jnp.int32, (rows, LANE), 1) < HDIM


def third(p, n):
    return pl.ds(mo(n * D + p * LANE, LANE), LANE)


def project_block(j, fa, gain, shift, bias, wq, qkv, normed, tokens):
    at = pl.ds(mo(j * tokens, 16), tokens)
    normal, _ = normalize(fa[at, :].astype(F32))
    normed[...] = (normal * gain[...] + shift[...]).astype(BF)

    def body(n):
        col = pl.ds(mo(n * 256, 256), 256)
        qkv[at, col] = (nn(normed[...], wq[:, col]) + bias[0:1, col]).astype(BF)
    loop(3 * D // 256, body)


def attend_pair(p, g, qkv, attended, stats, tokens):
    col = third(p, 0)
    query = qkv[pl.ds(mo(g * tokens, 16), tokens), col] * jnp.asarray(HDIM**-0.5, BF)
    keys, values = qkv[:, third(p, 1)], qkv[:, third(p, 2)]
    mask = head_mask(tokens)
    zero = jnp.zeros_like(query)
    lanes = lax.broadcasted_iota(jnp.int32, (tokens, LANE), 1)
    results = []
    for side in range(2):
        scores = nt(jnp.where(mask, query, zero) if side == 0 else jnp.where(mask, zero, query), keys)
        highest = jnp.max(scores, axis=-1, keepdims=True)
        shares = jnp.exp(scores - highest)
        total = jnp.sum(shares, axis=-1, keepdims=True)
        results.append(nn(shares.astype(BF), values) * (1.0 / total))
        stats[...] = jnp.where(lanes == 2 * p + side, highest + jnp.log(total), stats[...])
    attended[:, col] = jnp.where(mask, results[0], results[1]).astype(BF)


def query_back(p, g, qkv, a_all, stats, pgrad, v_qv, tokens):
    col = pl.ds(mo(p * LANE, LANE), LANE)
    own = pl.ds(mo(g * tokens, 16), tokens)
    scale = jnp.asarray(HDIM**-0.5, BF)
    query, upstream = qkv[own, col] * scale, a_all[own, col]
    keys, values = qkv[:, third(p, 1)], qkv[:, third(p, 2)]
    mask = head_mask(tokens)
    zero = jnp.zeros_like(query)
    lanes = lax.broadcasted_iota(jnp.int32, (tokens, LANE), 1)
    results = []
    for side in range(2):
        def pick(v):
            return jnp.where(mask, v, zero) if side == 0 else jnp.where(mask, zero, v)
        total = jnp.sum(jnp.where(lanes == 2 * p + side, stats[...], 0.0), axis=-1, keepdims=True)
        centre = jnp.sum(jnp.where(lanes == HEADS + 2 * p + side, stats[...], 0.0), axis=-1, keepdims=True)
        shares = jnp.exp(nt(pick(query), keys) - total)
        back = (shares * (nt(pick(upstream), values) - centre)).astype(BF) * scale
        results.append(nn(back, keys))
    grad = jnp.where(mask, results[0], results[1])
    pgrad[:, col] = grad.astype(BF)
    v_qv[0:1, col] = jnp.sum(grad, axis=0, keepdims=True)


def key_back(p, g, qkv, a_all, rows, pgrad, v_qv, tokens):
    col = pl.ds(mo(p * LANE, LANE), LANE)
    own = pl.ds(mo(g * tokens, 16), tokens)
    scale = jnp.asarray(HDIM**-0.5, BF)
    keys, values = qkv[own, third(p, 1)] * scale, qkv[own, third(p, 2)]
    queries, upstream = qkv[:, col], a_all[:, col]
    mask = head_mask(tokens)
    zero = jnp.zeros_like(keys)
    ks, vs = [], []
    for side in range(2):
        def pick(v):
            return jnp.where(mask, v, zero) if side == 0 else jnp.where(mask, zero, v)
        total = rows[pl.ds(2 * p + side, 1), :]
        centre = rows[pl.ds(HEADS + 2 * p + side, 1), :]
        shares = jnp.exp(nt(pick(keys), queries) - total)
        vs.append(nn(shares.astype(BF), upstream))
        back = (shares * (nt(pick(values), upstream) - centre)).astype(BF) * scale
        ks.append(nn(back, queries))
    pgrad[:, pl.ds(mo(D + p * LANE, LANE), LANE)] = jnp.where(mask, ks[0], ks[1]).astype(BF)
    grad = jnp.where(mask, vs[0], vs[1])
    pgrad[:, pl.ds(mo(2 * D + p * LANE, LANE), LANE)] = grad.astype(BF)
    v_qv[0:1, pl.ds(mo(D + p * LANE, LANE), LANE)] = jnp.sum(grad, axis=0, keepdims=True)


def cell(ref, m, row, sub=None):
    r0, rn, c0, cn = m.sub[sub] if sub is not None else (0, m.quarter, 0, m.half)
    return ref.at[pl.ds(mo(row + r0, 16), rn), pl.ds(c0, cn)]


ORDER = (3, 2, 1, 0)


def layer_kernel(groups, highs, names, fr, ct, p_ref, oq, oo, ou, od, osm, out_frames, frames_grad, *scratch):
    s = types.SimpleNamespace(**dict(zip(names, scratch)))
    rep, g = lax.axis_index("rep"), lax.axis_index("grp")
    tokens = fr.shape[0]
    share_of = lax.rem(rep, 8)
    h = lax.rem(share_of, 2)
    k = share_of // 2
    x, y = lax.rem(k, 2), k // 2
    kx, ky, kd = flip(k, 1), flip(k, 2), 3 - k
    core, xn, yn = flip(rep, 1), flip(rep, 2), flip(rep, 4)
    full = (s.wq, s.wo, s.wu, s.wd)
    outs = (oq, oo, ou, od)
    grads = (s.wu, s.go, s.gu, s.gd)
    last = groups - 1

    def has_next(d):
        return g < last if d == 0 else g > 0

    def toward(d):
        return lax.rem(g + (1 if d == 0 else last), groups)

    def row_of(d, step):
        return g - 1 - step if d == 0 else g + 1 + step

    def valid(d, step):
        return row_of(d, step) >= 0 if d == 0 else row_of(d, step) <= last

    slots = [(d, step) for step in range(last) for d in range(2)]

    def slot_of(d, step):
        return step if d else last - 1 - step

    def sent(region, sem):
        remote(region, region, sem, s.smr.at[0], core, g).wait_send()

    def arrived(region, sem):
        pltpu.make_async_copy(region, region, sem).wait()

    def piece_load(t, i, slot):
        m = MATS[t]
        count = (m.quarter * m.tiles + (2 if m.shifted else 0)) * LANE
        start = mo((m.row0 + lax.rem(k + i, 4) * (m.quarter * m.tiles)) * LANE, LANE)
        return pltpu.make_async_copy(p_ref.at[:, pl.ds(start, count)], s.pbuf.at[slot, :, pl.ds(0, count)], s.lsem.at[slot])

    def relayout(t, i, slot):
        m = MATS[t]
        piece_load(t, i, slot).wait()
        count = m.quarter * m.tiles + (8 if m.shifted else 0)
        s.fbuf[0:count, :] = s.pbuf[slot, :, 0:count * LANE].astype(F32).reshape(count, LANE)
        at = pl.ds(mo(g * m.block + lax.rem(k + i, 4) * m.quarter, 16), m.quarter)
        low = lax.broadcasted_iota(jnp.int32, (m.quarter, LANE), 1) < 64
        for c in range(m.tiles):
            a = s.fbuf[pl.ds(c, m.quarter, stride=m.tiles), :]
            if m.shifted:
                b = s.fbuf[pl.ds(c + 1, m.quarter, stride=m.tiles), :]
                a = pltpu.roll(jnp.where(low, b, a), 64, 1)
            full[t][at, c * LANE:(c + 1) * LANE] = a.astype(BF)

    def rest_load(t):
        for i in range(3):
            piece_load(t, i + 1, i).start()

    def rest(t):
        loop(3, lambda i: relayout(t, i + 1, i))

    def small_loads():
        at, result = 0, []
        for first, count in SMALL:
            result.append(pltpu.make_async_copy(
                p_ref.at[:, pl.ds(first * LANE, count * LANE)], s.spbuf.at[:, pl.ds(at * LANE, count * LANE)], s.ssem.at[0]))
            at += count
        return result

    def zregion(t, r):
        if t == 4:
            return s.fa.at[pl.ds(mo(r * tokens, 16), tokens), :]
        return part(full[t], MATS[t], r, k, h)

    def zcopy(t, d, step, r):
        reg = zregion(t, r)
        send = s.zs.at[t] if t < 4 else s.zfs.at[d, step]
        return remote(reg, reg, send, s.zr.at[t, slot_of(d, step)], rep, toward(d))

    def own_send(t):
        for d in range(2):
            @pl.when(has_next(d))
            def _():
                zcopy(t, d, 0, g).start()

    def xcopy(t, i, r, kk):
        reg = part(full[t], MATS[t], r, kk, h)
        return remote(reg, reg, s.gs.at[t, i], s.xr.at[t, i], xn, g)

    def ycopy(t, i, r, kk):
        reg = part(full[t], MATS[t], r, kk, h)
        return remote(reg, reg, s.gs.at[t, i], s.yr.at[t, i], yn, g)

    def acopy(t, i, r, kk):
        reg = part(full[t], MATS[t], r, kk, h, 0)
        return remote(reg, reg, s.gs.at[t, i], s.fr.at[t, i], yn, g)

    def bcopy(t, i, r, kk):
        reg = part(full[t], MATS[t], r, kk, h, 1)
        return remote(reg, reg, s.gs.at[t, i], s.fr.at[t, i], xn, g)

    def ccopy(t, i, r, hh):
        reg = slab(full[t], MATS[t], r, hh)
        return remote(reg, reg, s.gs.at[t, i], s.cr.at[t, i], core, g)

    def stage(number, t, d, step):
        i = slot_of(d, step)

        @pl.when(valid(d, step))
        def _():
            r = row_of(d, step)
            if number == 0:
                zcopy(t, d, step, r).wait_recv()
                if step < last - 1:
                    @pl.when(has_next(d))
                    def _():
                        zcopy(t, d, step + 1, r).start()
                if t < 4:
                    xcopy(t, i, r, k).start()
                    ycopy(t, i, r, k).start()
            if number == 1:
                xcopy(t, i, r, kx).wait_recv()
                acopy(t, i, r, kx).start()
                ycopy(t, i, r, ky).wait_recv()
                bcopy(t, i, r, ky).start()
            if number == 2:
                arrived(part(full[t], MATS[t], r, kd, h), s.fr.at[t, i])
                ccopy(t, i, r, h).start()
            if number == 3:
                ccopy(t, i, r, 1 - h).wait_recv()

    def both(number, t, step):
        for d in range(2):
            stage(number, t, d, step)

    def gather_sent():
        inner = jnp.logical_and(g > 0, g < last)
        for t in range(4):
            m = MATS[t]

            @pl.when(inner)
            def _():
                sent(full[t].at[pl.ds(0, (2 + last) * m.quarter), pl.ds(0, m.half)], s.zs.at[t])

            @pl.when(jnp.logical_not(inner))
            def _():
                sent(full[t].at[pl.ds(0, m.quarter), pl.ds(0, m.half)], s.zs.at[t])
            for i in range(last):
                sent(full[t].at[pl.ds(0, 7 * m.quarter), pl.ds(0, m.half)], s.gs.at[t, i])
        for d in range(2):
            @pl.when(has_next(d))
            def _():
                zcopy(4, d, 0, g).wait_send()
            for step in range(last - 1):
                @pl.when(jnp.logical_and(valid(d, step), has_next(d)))
                def _():
                    zcopy(4, d, step + 1, g).wait_send()

    def vcopy(i, owner):
        return remote(s.smb, s.sm.at[owner], s.ms.at[0], s.mr.at[0], rep, lax.rem(g + i, groups))

    def place(r):
        return s.a_all.at[pl.ds(mo(r * tokens, 16), tokens), :]

    def scopy(d, step, r):
        return remote(place(r), place(r), s.szs.at[d, step], s.szr.at[slot_of(d, step)], rep, toward(d))

    def rcopy(i, owner):
        return remote(s.rows3.at[groups], s.rows3.at[owner], s.rs.at[0], s.rr.at[0], rep, lax.rem(g + i, groups))

    def share_start():
        for d in range(2):
            @pl.when(has_next(d))
            def _():
                scopy(d, 0, g).start()
        for i in range(1, groups):
            rcopy(i, g).start()

    def share_step(step):
        for d in range(2):
            @pl.when(valid(d, step))
            def _():
                r = row_of(d, step)
                scopy(d, step, r).wait_recv()
                if step < last - 1:
                    @pl.when(has_next(d))
                    def _():
                        scopy(d, step + 1, r).start()

    def share_rows():
        arrived(s.rows3.at[pl.ds(0, last)], s.rr.at[0])
        for i in range(groups):
            s.rows[:, i * tokens:(i + 1) * tokens] = s.rows3[i]
        s.rows[:, pl.ds(mo(g * tokens, LANE), tokens)] = s.rows3[groups]

    def share_sent():
        for d in range(2):
            @pl.when(has_next(d))
            def _():
                scopy(d, 0, g).wait_send()
            for step in range(last - 1):
                @pl.when(jnp.logical_and(valid(d, step), has_next(d)))
                def _():
                    scopy(d, step + 1, g).wait_send()
        sent(s.rows3.at[pl.ds(0, last)], s.rs.at[0])

    def row(i):
        return lax.rem(g + 1 + i, groups)

    def first(t, i):
        m = MATS[t]
        at = pl.ds(mo(row(i) * m.block, 16), m.block)
        return remote(grads[t].at[at, pl.ds(mo((1 - h) * m.half, LANE), m.half)], s.buf1[t].at[at, :],
                      s.gone.at[t, i], s.c1r.at[t, i], core, g)

    def cell1(t, i, kk, sub=None):
        return cell(s.buf1[t], MATS[t], row(i) * MATS[t].block + kk * MATS[t].quarter, sub)

    def cell2(t, i, j, sub):
        return cell(s.buf2[t], MATS[t], (row(i) * 2 + j) * MATS[t].quarter, sub)

    def cell3(t, i, sub=None):
        return cell(s.buf3[t], MATS[t], row(i) * MATS[t].quarter, sub)

    def a1(t, i, j, kk):
        return remote(cell1(t, i, kk, 0), cell2(t, i, j, 0), s.gone.at[t, i], s.ab1r.at[t, i], xn, g)

    def b1(t, i, j, kk):
        return remote(cell1(t, i, kk, 1), cell2(t, i, j, 1), s.gone.at[t, i], s.ab1r.at[t, i], yn, g)

    def a2(t, i, j):
        return remote(cell2(t, i, j, 0), cell3(t, i, 0), s.gone.at[t, i], s.ab2r.at[t, i], yn, g)

    def b2(t, i, j):
        return remote(cell2(t, i, j, 1), cell3(t, i, 1), s.gone.at[t, i], s.ab2r.at[t, i], xn, g)

    def z2(t, i):
        slot = (1 - lax.rem(g, 2)) if i == 0 else lax.rem(g, 2)
        return remote(cell3(t, i), s.zbuf[t].at[slot], s.gone.at[t, i], s.z2r.at[t, slot], rep, flip(g, 1))

    def z2_got(t, slot):
        arrived(s.zbuf[t].at[slot], s.z2r.at[t, slot])

    def z3(t):
        return remote(cell3(t, 1), s.zbuf[t].at[2], s.gone.at[t, 1], s.z2r.at[t, 2], rep, flip(g, 2))

    def r1(t, i):
        m = MATS[t]
        first(t, i).wait_recv()
        at = pl.ds(mo(row(i) * m.block, 16), m.block)
        mine = grads[t].at[at, pl.ds(mo(h * m.half, LANE), m.half)]
        add_rows(s.buf1[t].at[at, :], mine, s.buf1[t].at[at, :], m.block)
        for j in range(2):
            a1(t, i, j, 2 * j + (1 - x)).start()
            b1(t, i, j, 2 * (1 - y) + j).start()

    def r2(t, i):
        m = MATS[t]
        arrived(s.buf2[t].at[pl.ds(mo(row(i) * 2 * m.quarter, 16), 2 * m.quarter), :], s.ab1r.at[t, i])
        for j in range(2):
            add_rows(cell2(t, i, j, 0), cell1(t, i, 2 * j + x, 0), cell2(t, i, j, 0), m.sub[0][1])
        a2(t, i, 1 - y).start()
        for j in range(2):
            add_rows(cell2(t, i, j, 1), cell1(t, i, 2 * y + j, 1), cell2(t, i, j, 1), m.sub[1][1])
        b2(t, i, 1 - x).start()

    def r3(t, i):
        m = MATS[t]
        arrived(cell3(t, i), s.ab2r.at[t, i])
        add_rows(cell3(t, i, 0), cell2(t, i, y, 0), cell3(t, i, 0), m.sub[0][1])
        add_rows(cell3(t, i, 1), cell2(t, i, x, 1), cell3(t, i, 1), m.sub[1][1])
        if i % 2 == 0:
            z2(t, i).start()

    def r3b(t):
        z2_got(t, 0)
        add_rows(cell3(t, 1), cell3(t, 1), s.zbuf[t].at[0], MATS[t].quarter)
        z3(t).start()

    def fpart(t, kk, hh, sub=None):
        return part(outs[t], MATS[t], 0, kk, hh, sub)

    def keep(t):
        return pltpu.make_async_copy(s.fin[t].at[0], fpart(t, k, h), s.os.at[t])

    def xsend(t):
        return remote(s.fin[t].at[0], fpart(t, k, h), s.osent.at[t], s.oxr.at[t], xn, g)

    def ysend(t):
        return remote(s.fin[t].at[0], fpart(t, k, h), s.osent.at[t], s.oyr.at[t], yn, g)

    def xgot(t):
        return remote(fpart(t, kx, h), fpart(t, kx, h), s.osent.at[t], s.oxr.at[t], xn, g)

    def ygot(t):
        return remote(fpart(t, ky, h), fpart(t, ky, h), s.osent.at[t], s.oyr.at[t], yn, g)

    def fwd(t, sub, kk):
        reg = fpart(t, kk, h, sub)
        return remote(reg, reg, s.osent.at[t], s.oar.at[t], (yn, xn)[sub], g)

    def cross(t, hh):
        reg = slab(outs[t], MATS[t], 0, hh)
        return remote(reg, reg, s.osent.at[t], s.ocr.at[t], core, g)

    def r4(t):
        m = MATS[t]
        z2_got(t, 1)
        z3(t).wait_recv()
        mine = cell3(t, last)

        def body(n):
            at = pl.ds(mo(n * 16, 16), 16)
            total = mine[at, :].astype(F32) + s.zbuf[t][1, at, :].astype(F32) + s.zbuf[t][2, at, :].astype(F32)
            s.fin[t][0, at, :] = total.astype(BF)
        loop(m.quarter // 16, body)
        for b in range(highs):
            cp = remote(s.fin[t].at[0], s.fin[t].at[1 + b], s.fxs.at[t, b], s.fxr.at[t, b], flip(rep, 8 << b), g)
            cp.start()
            cp.wait()
            add_rows(s.fin[t].at[0], s.fin[t].at[0], s.fin[t].at[1 + b], m.quarter)
        keep(t).start()
        xsend(t).start()
        ysend(t).start()

    def r5(t):
        xgot(t).wait_recv()
        fwd(t, 0, kx).start()
        ygot(t).wait_recv()
        fwd(t, 1, ky).start()

    def r6(t):
        arrived(fpart(t, kd, h), s.oar.at[t])
        keep(t).wait()
        cross(t, h).start()

    partners = [(core, g), (xn, g), (yn, g)] + [(flip(rep, 8 << b), g) for b in range(highs)]
    bit = 1
    while bit < groups:
        partners.append((rep, flip(g, bit)))
        bit *= 2

    def smcopy(j):
        return remote(s.smacc.at[j], s.smin.at[j], s.sms.at[j], s.smr.at[j], *partners[j])

    def small(j):
        if j:
            smcopy(j - 1).wait_recv()
            s.smacc[j] = s.smacc[j - 1] + s.smin[j - 1]
        if j < len(partners):
            smcopy(j).start()
        else:
            osm[...] = s.smacc[j, g]

    def crossed():
        for t in ORDER:
            cross(t, 1 - h).wait_recv()

    def chunks_sent():
        for t in ORDER:
            m = MATS[t]
            for i in range(groups):
                sent(grads[t].at[pl.ds(0, (8 if i < last else 7) * m.quarter), pl.ds(0, m.half)], s.gone.at[t, i])

    def outs_sent():
        sent(s.sm.at[pl.ds(0, last)], s.ms.at[0])
        for t in ORDER:
            m = MATS[t]
            sent(grads[t].at[pl.ds(0, 7 * m.quarter), pl.ds(0, m.half)], s.osent.at[t])
        for j in range(len(partners)):
            smcopy(j).wait_send()

    def project(j):
        project_block(j, s.fa, s.gain1, s.shift1, s.bias3, s.wq, s.qkv, s.normed, tokens)

    def attention(p):
        loop(2, lambda i: attend_pair(p + i, g, s.qkv, s.attended, s.stats, tokens))

    def block(n):
        return pl.ds(mo(n * 256, 256), 256)

    def to_middle():
        def body(n):
            c = block(n)
            s.middle[:, c] = nn(s.attended[...], s.wo[:, c]) + s.obias[0:1, c] + fr[:, c].astype(F32)
        loop(D // 256, body)
        value, inverse = normalize(s.middle[...])
        s.normal[...] = value
        s.inverse[...] = jnp.broadcast_to(inverse, (tokens, LANE))
        s.normed[...] = (value * s.gain2[...] + s.shift2[...]).astype(BF)

    def hidden(i):
        def body(j):
            n = row(i) * (FF // 256 // groups) + j
            c = block(n)
            u = nn(s.normed[...], s.wu[:, c]) + s.ubias[0:1, c]
            bell = 0.5 * (1.0 + lax.erf(u * ROOT_HALF))
            s.act[:, c] = (u * bell).astype(BF)
            slope = bell + u * jnp.exp(-0.5 * u * u) * ROOT_TWO_PI
            grad = nt(ct[...], s.wd[block(n), :]) * slope
            s.v_up[0:1, c] = jnp.sum(grad, axis=0, keepdims=True)
            s.pre[:, c] = grad.astype(BF)
        loop(FF // 256 // groups, body)

    def to_output():
        def body(n):
            c = block(n)
            out_frames[:, c] = (nn(s.act[...], s.wd[:, c]) + s.dbias[0:1, c] + s.middle[:, c]).astype(BF)
        loop(D // 256, body)

    def back_up():
        def body(n):
            s.wide[:, block(n)] = nt(s.pre[...], s.wu[block(n), :])
        loop(D // 256, body)

    def back_norm():
        upstream, normal = s.wide[...], s.normal[...]
        s.v_gain2[...] = jnp.sum(upstream * normal, axis=0, keepdims=True)
        s.v_shift2[...] = jnp.sum(upstream, axis=0, keepdims=True)
        total = ct[...].astype(F32) + norm_back(upstream, normal, s.inverse[:, 0:1], s.gain2[...])
        s.mgrad[...] = total
        s.half[...] = total.astype(BF)
        s.v_out[...] = jnp.sum(total, axis=0, keepdims=True)
        s.v_down[...] = jnp.sum(ct[...].astype(F32), axis=0, keepdims=True)

        def body(n):
            s.a_all[own, block(n)] = nt(s.half[...], s.wo[block(n), :]).astype(BF)
        own = pl.ds(mo(g * tokens, 16), tokens)
        loop(D // 256, body)
        lanes = lax.broadcasted_iota(jnp.int32, (tokens, LANE), 1)
        mask = head_mask(tokens)
        stats = s.stats[...]
        for p in range(HEADS // 2):
            c = slice(p * LANE, (p + 1) * LANE)
            product = s.a_all[own, c].astype(F32) * s.attended[:, c].astype(F32)
            for side in range(2):
                mine = jnp.where(mask if side == 0 else jnp.logical_not(mask), product, 0.0)
                stats = jnp.where(lanes == HEADS + 2 * p + side, jnp.sum(mine, axis=-1, keepdims=True), stats)
        s.stats[...] = stats
        s.rows3[groups] = stats.T[0:2 * HEADS, :]

    def weight(t, i, left, right):
        m = MATS[t]
        s.turned[0:m.block, :] = left[:, pl.ds(mo(row(i) * m.block, LANE if m.block % LANE == 0 else 64), m.block)].T

        def body(n):
            c = block(n)
            grads[t][pl.ds(mo(row(i) * m.block, 16), m.block), c] = nn(s.turned[0:m.block, :], right[:, c]).astype(BF)
        loop(m.cols // 256, body)
        first(t, i).start()

    def turn(left, out):
        out[...] = left[...].T

    def weight_all(t, left, right):
        def body(n):
            c = block(n)
            grads[t][:, c] = nn(left[...], right[:, c]).astype(BF)
        loop(MATS[t].cols // 256, body)
        for i in (0, 2, 1, 3):
            first(t, i).start()

    def queries(p):
        loop(2, lambda i: query_back(p + i, g, s.qkv, s.a_all, s.stats, s.pgrad, s.v_qv, tokens))

    def keys(p):
        loop(2, lambda i: key_back(p + i, g, s.qkv, s.a_all, s.rows, s.pgrad, s.v_qv, tokens))

    def to_inputs():
        normal, _ = normalize(fr[...].astype(F32))
        s.normed[...] = (normal * s.gain1[...] + s.shift1[...]).astype(BF)
        turn(s.normed, s.turned)

    def input_grad():
        def body(n):
            s.wide[:, block(n)] = nt(s.pgrad[...], s.wq[block(n), :])
        loop(D // 256, body)
        normal, inverse = normalize(fr[...].astype(F32))
        upstream = s.wide[...]
        s.v_gain1[...] = jnp.sum(upstream * normal, axis=0, keepdims=True)
        s.v_shift1[...] = jnp.sum(upstream, axis=0, keepdims=True)
        frames_grad[...] = (s.mgrad[...] + norm_back(upstream, normal, inverse, s.gain1[...])).astype(BF)
        fill_image(s.smacc.at[0], range(SROWS), (
            (GAIN_ONE, s.v_gain1), (SHIFT_ONE, s.v_shift1), (QV_BIAS, s.v_qv), (OUT_BIAS, s.v_out), (GAIN_TWO, s.v_gain2),
            (SHIFT_TWO, s.v_shift2), (UP_BIAS, s.v_up), (DOWN_BIAS, s.v_down)))
        small(0)

    barrier, peers = greet(rep, g, groups)
    peers += [(flip(rep, 8 << b), g) for b in range(highs)]
    for t in range(3):
        piece_load(t, 0, t).start()
    for cp in small_loads():
        cp.start()
    own_frames = pltpu.make_async_copy(fr, zregion(4, g), s.ssem.at[1])
    own_frames.start()
    do_barrier(barrier, peers)
    relayout(0, 0, 0)
    own_send(0)
    piece_load(3, 0, 0).start()
    relayout(1, 0, 1)
    own_send(1)
    relayout(2, 0, 2)
    own_send(2)
    pltpu.make_async_copy(s.spbuf, s.spbuf, s.ssem.at[0]).wait()
    s.smb[...] = jnp.zeros_like(s.smb)
    count = sum(c for _, c in SMALL)
    s.smb[0:count, :] = s.spbuf[...].astype(F32).reshape(count, LANE)
    for i in range(1, groups):
        vcopy(i, g).start()
    both(0, 0, 0)
    both(0, 0, 1)
    own_frames.wait()
    own_send(4)
    relayout(3, 0, 0)
    own_send(3)
    rest_load(0)
    rest(0)
    rest_load(1)
    both(0, 0, 2)
    both(1, 0, 0)
    both(1, 0, 1)
    both(0, 1, 0)
    both(0, 2, 0)
    both(1, 0, 2)
    both(2, 0, 0)
    both(2, 0, 1)
    rest(1)
    rest_load(2)
    both(2, 0, 2)
    arrived(s.sm.at[pl.ds(0, last)], s.mr.at[0])
    s.sm[g] = s.smb[...]
    for spot, ref in ((GAIN_ONE, s.gain1), (SHIFT_ONE, s.shift1), (QV_BIAS, s.qvbias), (GAIN_TWO, s.gain2), (SHIFT_TWO, s.shift2),
                      (OUT_BIAS, s.obias), (UP_BIAS, s.ubias), (DOWN_BIAS, s.dbias)):
        assemble(s.sm, spot, ref)
    s.bias3[...] = jnp.zeros_like(s.bias3)
    s.bias3[0:1, 0:D] = s.qvbias[0:1, 0:D]
    s.bias3[0:1, 2 * D:3 * D] = s.qvbias[0:1, D:2 * D]
    s.stats[...] = jnp.zeros_like(s.stats)
    both(0, 4, 0)
    rest(2)
    rest_load(3)
    both(1, 1, 0)
    both(1, 2, 0)
    for step in range(last):
        both(3, 0, step)
    project(g)
    both(0, 3, 0)

    def project_rows(step):
        def body(d):
            r = g + (2 * d - 1) * (1 + step)

            @pl.when(jnp.logical_and(r >= 0, r <= last))
            def _():
                project(r)
        loop(2, body)
    project_rows(0)
    both(0, 4, 1)
    rest(3)
    both(2, 1, 0)
    both(2, 2, 0)
    both(1, 3, 0)
    both(0, 1, 1)
    both(0, 2, 1)
    project_rows(1)
    both(0, 3, 1)
    both(2, 3, 0)
    both(1, 1, 1)
    both(1, 2, 1)
    both(0, 4, 2)
    project_rows(2)
    both(0, 1, 2)
    both(1, 3, 1)
    both(2, 1, 1)
    both(2, 2, 1)
    both(0, 2, 2)
    attention(0)
    both(0, 3, 2)
    both(1, 1, 2)
    both(2, 3, 1)
    attention(2)
    both(1, 2, 2)
    attention(4)
    both(1, 3, 2)
    both(2, 1, 2)
    both(2, 2, 2)
    both(2, 3, 2)
    rest = [(t, step) for step in range(last) for t in (1, 2, 3)]
    for t, step in rest:
        if t == 1:
            both(3, t, step)
    to_middle()
    for t, step in rest:
        if t > 1:
            both(3, t, step)
    hidden(0)
    weight(3, 0, s.act, ct)
    hidden(1)
    hidden(2)
    r1(3, 0)
    hidden(3)
    back_up()
    back_norm()
    share_start()
    weight(3, 2, s.act, ct)
    r2(3, 0)
    weight(3, 1, s.act, ct)
    r1(3, 2)
    weight(3, 3, s.act, ct)
    r1(3, 1)
    turn(s.normed, s.turned2)
    r1(3, 3)
    r2(3, 2)
    weight_all(2, s.turned2, s.pre)
    r2(3, 1)
    r1(2, 0)
    to_output()
    share_step(0)
    r1(2, 2)
    r2(3, 3)
    turn(s.attended, s.turned2)
    weight_all(1, s.turned2, s.half)
    gather_sent()
    r2(2, 0)
    r1(2, 1)
    queries(0)
    share_step(1)
    r2(2, 2)
    r1(2, 3)
    queries(2)
    queries(4)
    r2(2, 1)
    r1(1, 0)
    r1(1, 2)
    share_step(2)
    share_rows()
    r3(3, 0)
    r3(3, 2)
    keys(0)
    r2(2, 3)
    r1(1, 1)
    r1(1, 3)
    r3(3, 1)
    r3(3, 3)
    r2(1, 0)
    r2(1, 2)
    to_inputs()
    keys(2)
    r2(1, 1)
    r2(1, 3)
    keys(4)
    r3b(3)
    r3(2, 0)
    r3(2, 2)
    weight_all(0, s.turned, s.pgrad)
    r3(2, 1)
    r3(2, 3)
    input_grad()
    r1(0, 0)
    r1(0, 2)
    r4(3)
    r2(0, 0)
    r2(0, 2)
    r1(0, 1)
    r1(0, 3)
    r3(1, 0)
    r3(1, 2)
    r3b(2)
    r3(0, 0)
    r3(0, 2)
    r5(3)
    r2(0, 1)
    small(1)
    r3(1, 1)
    r3(1, 3)
    r2(0, 3)
    r4(2)
    r6(3)
    r3b(1)
    r3(0, 1)
    r3(0, 3)
    r3b(0)
    r5(2)
    r4(1)
    small(2)
    r6(2)
    r4(0)
    r5(1)
    small(3)
    r5(0)
    small(4)
    r6(1)
    r6(0)
    for j in range(5, len(partners) + 1):
        small(j)
    crossed()
    share_sent()
    chunks_sent()
    outs_sent()


def layer(frames, cotangent, params, groups, reps):
    dma = pltpu.SemaphoreType.DMA
    tokens = frames.shape[0]
    clip = tokens * groups
    highs = (reps // 8).bit_length() - 1
    steps = 3 + highs + groups.bit_length() - 1
    n = 2 * (groups - 1)

    def bf(*shape):
        return pltpu.VMEM(shape, BF)

    def wide(*shape):
        return pltpu.VMEM(shape, F32)

    scratch = {name: bf(m.block * groups, m.cols) for name, m in zip(("wq", "wo", "wu", "wd"), MATS)}
    scratch.update(go=bf(D, D), gu=bf(D, FF), gd=bf(FF, D))
    scratch.update(buf1=[bf(m.block * groups, m.half) for m in MATS], buf2=[bf(m.quarter * groups * 2, m.half) for m in MATS],
                   buf3=[bf(m.quarter * groups, m.half) for m in MATS], zbuf=[bf(groups - 1, m.quarter, m.half) for m in MATS],
                   fin=[bf(highs + 1, m.quarter, m.half) for m in MATS])
    scratch.update(fa=bf(clip, D), qkv=bf(clip, 3 * D), a_all=bf(clip, D))
    scratch.update(attended=bf(tokens, D), normed=bf(tokens, D), half=bf(tokens, D),
                   act=bf(tokens, FF), pre=bf(tokens, FF), pgrad=bf(tokens, 3 * D), turned=bf(D, tokens), turned2=bf(D, tokens))
    scratch.update(middle=wide(tokens, D), normal=wide(tokens, D), mgrad=wide(tokens, D), wide=wide(tokens, D),
                   inverse=wide(tokens, LANE), stats=wide(tokens, LANE))
    scratch.update(rows3=wide(groups + 1, 2 * HEADS, tokens), rows=wide(2 * HEADS, clip))
    scratch.update({name: wide(1, D) for name in ("gain1", "shift1", "gain2", "shift2", "obias", "dbias", "v_gain1", "v_shift1",
                                                  "v_gain2", "v_shift2", "v_out", "v_down")})
    scratch.update(qvbias=wide(1, 2 * D), bias3=wide(1, 3 * D), v_qv=wide(1, 2 * D), ubias=wide(1, FF), v_up=wide(1, FF))
    piece = max(m.quarter * m.tiles + 8 for m in MATS)
    scratch.update(pbuf=bf(3, 1, piece * LANE), fbuf=wide(piece, LANE), spbuf=bf(1, sum(c for _, c in SMALL) * LANE),
                   smb=wide(SROWS, LANE), sm=wide(groups, SROWS, LANE),
                   smacc=wide(steps + 1, groups, SROWS, LANE), smin=wide(steps, groups, SROWS, LANE))
    scratch.update(lsem=dma((3,)), ssem=dma((2,)), zs=dma((4,)), zfs=dma((2, groups - 1)), zr=dma((5, groups - 1)))
    scratch.update({name: dma((4, groups - 1)) for name in ("gs", "xr", "yr", "fr", "cr", "z2r")})
    scratch.update({name: dma((1,)) for name in ("ms", "mr", "rs", "rr")})
    scratch.update(szs=dma((2, groups - 1)), szr=dma((groups - 1,)))
    scratch.update({name: dma((4, groups)) for name in ("gone", "c1r", "ab1r", "ab2r")})
    if highs:
        scratch.update({name: dma((4, highs)) for name in ("fxs", "fxr")})
    scratch.update({name: dma((4,)) for name in ("os", "osent", "oxr", "oyr", "oar", "ocr")})
    scratch.update(sms=dma((steps,)), smr=dma((steps,)))
    vmem, hbm = pl.BlockSpec(memory_space=pltpu.VMEM), pl.BlockSpec(memory_space=pl.ANY)
    sds = jax.ShapeDtypeStruct
    names = tuple(scratch)
    flat, tree = jax.tree.flatten(list(scratch.values()))

    def body(*refs):
        fixed = 10
        layer_kernel(groups, highs, names, *refs[:fixed], *jax.tree.unflatten(tree, refs[fixed:]))

    return pl.pallas_call(
        body,
        out_shape=[sds((m.block, m.cols), BF) for m in MATS] + [sds((SROWS, LANE), F32), sds((tokens, D), BF), sds((tokens, D), BF)],
        in_specs=[vmem, vmem, hbm],
        out_specs=[hbm] * 4 + [vmem] * 3,
        scratch_shapes=flat,
        compiler_params=pltpu.CompilerParams(collective_id=0, has_side_effects=True, vmem_limit_bytes=67043328),
        name="layer",
    )(frames, cotangent, params)


BETA_ONE = 0.9
BETA_TWO = 0.98
ADAM_EPS = 1e-06
LEARN_RATE = 0.006
DECAY = 0.01
ADAM_STEP = 4
ROWS = 1792
CHUNKS = -(-FROWS // ROWS)
SUB = 224


def flatten(m, block, flat, late):
    def body(i):
        base = m.row0 + i * (48 * m.tiles)
        for c in range(m.tiles):
            tile = block[pl.ds(mo(i * 48, 16), 48), c * LANE:(c + 1) * LANE].astype(F32)
            if m.shifted:
                tile = pltpu.roll(tile, 64, 1)
                late[pl.ds(base + c + 1, 48, stride=m.tiles), :] = tile
            flat[pl.ds(base + c, 48, stride=m.tiles), :] = tile
    loop(m.block // 48, body)


def adam_kernel(scale, gq, go, gu, gd, sm, p_hbm, m_hbm, v_hbm, fo, fg, o_g, o_p, o_m, o_v, o_fo, o_fg,
                bq, bo, bu, bd, flat, late, pb, mb, vb, gb, nb, frames, bsem, isem, osem, fsem):
    blocks = (bq, bo, bu, bd)

    def view(ref, c):
        return ref.at[:, pl.ds(c * ROWS * LANE, min(ROWS, FROWS - c * ROWS) * LANE)]

    loads = [pltpu.make_async_copy(a, b, bsem.at[i]) for i, (a, b) in enumerate(zip((gq, go, gu, gd), blocks))]
    pairs = ((p_hbm, pb), (m_hbm, mb), (v_hbm, vb))
    ins = [[pltpu.make_async_copy(view(a, c), view(b, c), isem.at[c, i]) for i, (a, b) in enumerate(pairs)] for c in range(CHUNKS)]
    results = ((gb, o_g), (nb, o_p), (mb, o_m), (vb, o_v))
    puts = [[pltpu.make_async_copy(view(a, c), view(b, c), osem.at[c, i]) for i, (a, b) in enumerate(results)] for c in range(CHUNKS)]
    takes = [pltpu.make_async_copy(a, frames.at[i], fsem.at[i]) for i, a in enumerate((fo, fg))]
    gives = [pltpu.make_async_copy(frames.at[i], a, fsem.at[2 + i]) for i, a in enumerate((o_fo, o_fg))]
    def fetch(c):
        if c < CHUNKS:
            for cp in ins[c]:
                cp.start()

    loads[0].start()
    fetch(0)
    loads[1].start()
    fetch(1)
    loads[2].start()

    def update(c):
        for cp in ins[c]:
            cp.wait()

        def body(j):
            start = c * ROWS + j * SUB
            at = pl.ds(mo(start, 8), SUB)
            lanes = (slice(None), pl.ds(mo(start * LANE, LANE), SUB * LANE))
            number = start + lax.broadcasted_iota(jnp.int32, (SUB, LANE), 0)
            low = lax.broadcasted_iota(jnp.int32, (SUB, LANE), 1) < 64
            grad = jnp.where(jnp.logical_and(number > UP.row0, low), late[at, :], flat[at, :]).reshape(1, SUB * LANE) * scale
            first = BETA_ONE * mb[lanes] + (1.0 - BETA_ONE) * grad
            second = BETA_TWO * vb[lanes] + (1.0 - BETA_TWO) * grad * grad
            gb[lanes] = grad
            mb[lanes] = first
            vb[lanes] = second
            first_hat = first * (1.0 / (1.0 - BETA_ONE**ADAM_STEP))
            second_hat = second * (1.0 / (1.0 - BETA_TWO**ADAM_STEP))
            current = pb[lanes].astype(F32)
            nb[lanes] = current - LEARN_RATE * (first_hat / (jnp.sqrt(second_hat) + ADAM_EPS) + DECAY * current)
        loop(-(-min(ROWS, FROWS - c * ROWS) // SUB), body)
        fetch(c + 2)
        for cp in puts[c]:
            cp.start()

    loads[0].wait()
    flatten(QKV, bq, flat, late)
    flat[0:3, :] = sm[0:3, :]
    update(0)
    loads[1].wait()
    flatten(OUT, bo, flat, late)
    flat[3459:3462, :] = sm[3:6, :]
    update(1)
    loads[2].wait()
    flatten(UP, bu, flat, late)
    flat[4614:4618, :] = sm[6:10, :]
    flat[4618:4619, 0:64] = sm[10:11, 0:64]
    flat[9226:9227, 64:128] = sm[11:12, 64:128]
    update(2)
    loads[3].start()
    for cp in takes:
        cp.start()
    update(3)
    update(4)
    loads[3].wait()
    flatten(DOWN, bd, flat, late)
    for ref in (flat, late):
        ref[9227:9232, :] = sm[12:17, :]
        ref[9232:9233, 0:64] = sm[17:18, 0:64]
        ref[13841:13842, :] = sm[19:20, :]
    flat[13840:13841, 64:128] = sm[18:19, 64:128]
    update(5)
    for cp in takes:
        cp.wait()
    for cp in gives:
        cp.start()
    for c in range(6, CHUNKS):
        update(c)
    for cp in gives:
        cp.wait()
    for chunk in puts:
        for cp in chunk:
            cp.wait()


def adam(blocks, smalls, params, first, second, reps, *outputs):
    vmem, hbm = pl.BlockSpec(memory_space=pltpu.VMEM), pl.BlockSpec(memory_space=pl.ANY)
    dma = pltpu.SemaphoreType.DMA
    row = pltpu.VMEM((1, CHUNKS * ROWS * LANE), F32)
    return pl.pallas_call(
        functools.partial(adam_kernel, 1.0 / reps),
        out_shape=[jax.ShapeDtypeStruct((1, FLAT), F32)] * 4 + [jax.ShapeDtypeStruct(o.shape, o.dtype) for o in outputs],
        in_specs=[hbm] * 4 + [vmem] + [hbm] * 5,
        out_specs=[hbm] * 6,
        scratch_shapes=[pltpu.VMEM(b.shape, BF) for b in blocks] + [pltpu.VMEM((CHUNKS * ROWS, LANE), F32)] * 2
        + [pltpu.VMEM((1, CHUNKS * ROWS * LANE), BF)] + [row] * 4 + [pltpu.VMEM((2,) + outputs[0].shape, BF)]
        + [dma((4,)), dma((CHUNKS, 3)), dma((CHUNKS, 4)), dma((4,))],
        compiler_params=pltpu.CompilerParams(vmem_limit_bytes=67043328),
        name="adam",
    )(*blocks, smalls, params, first, second, *outputs)


def on_device(frames, cotangent, params, first_moment, second_moment):
    groups, reps = lax.axis_size("grp"), lax.axis_size("rep")
    *blocks, small, out_frames, frames_grad = layer(frames, cotangent, params, groups, reps)
    param_grad, new_params, new_first, new_second, out_frames, frames_grad = adam(
        blocks, small, params, first_moment, second_moment, reps, out_frames, frames_grad)
    return (out_frames, frames_grad, param_grad, new_params, new_first, new_second)


def solution(mesh):
    in_specs = (
        P(("rep", "grp"), None),
        P(("rep", "grp"), None),
        P("grp", None),
        P("grp", None),
        P("grp", None),
    )
    out_specs = (
        P(("rep", "grp"), None),
        P(("rep", "grp"), None),
        P("grp", None),
        P("grp", None),
        P("grp", None),
        P("grp", None),
    )
    return jax.shard_map(
        on_device, mesh=mesh, in_specs=in_specs, out_specs=out_specs, check_vma=False
    )
```

profile of v0, /device:TPU:28, one launch (start us, length us, event | category | flops | bytes accessed | tf_op | source)
XLA Modules:
  0.0 201.7 jit_solution(4270965527750624964)
XLA Ops:
  0.6 176.9 %layer.1 = (bf16[192,2304]{1,0:T(8,128)(2,1)}, bf16[192,768]{1,0:T(8,128)(2,1)}, bf16[192,3072]{1,0:T(8,128)(2,1)}, bf16[768,768]{1,0:T(8,128)(2,1)}, f32[24,128...) custom-call(bf16[256,768]{1,0:T(8,128)(2,1)} %refs_0_.1, bf16[256,768]{1,0:T(8,128)(2,1)} %refs_1_.1, ...), custom_call_target="tpu_custom_call" | custom-call | tf_op jit(solution)/shard_map/layer/pallas_call | solution.py:1009
  177.6 24.0 %adam.1 = (f32[1,1771776]{1,0:T(1,128)}, f32[1,1771776]{1,0:T(1,128)}, f32[1,1771776]{1,0:T(1,128)}, f32[1,1771776]{1,0:T(1,128)}, bf16[256,768]{1,0:T(8,128)(2,1)}, /*index=5*/bf16[256,768]{1,0:T(8,128)(2,1)}) custom-call(bf16[192,2304]{1,0:T(8,128)(2,1)} %get-tuple-element.19.gq, bf16[192,768]{1,0:T(8,128)(2,1)} %get-tuple-element.20.go, ...), custom_call_target="tpu_custom_call" | custom-call | tf_op jit(solution)/shard_map/adam/pallas_call | solution.py:1137
where the time goes:
time: 204 us; the launch traced here: 202 us
  Pallas kernels  201 us (99%)
    pallas_call x1, Pallas kernels, layer(): pl.pallas_call(body, out_shape=[sds((m.block, m.cols), BF) for m in MATS]...  177 us
    pallas_call x1, Pallas kernels, adam(): pl.pallas_call(functools.partial(adam_kernel, 1.0 / reps), out_shape=[jax...  24 us

commit v1 on v0

--- a/solution.py
+++ b/solution.py
@@ -196,35 +196,38 @@
     attended[:, col] = jnp.where(mask, results[0], results[1]).astype(BF)
 
 
-def query_back(p, g, qkv, a_all, stats, pgrad, v_qv, tokens):
-    col = pl.ds(mo(p * LANE, LANE), LANE)
-    own = pl.ds(mo(g * tokens, 16), tokens)
+def query_back(w, p, j, qkv, upstream_all, cols, pgh, csum, tokens):
+    own = pl.ds(mo(j * tokens, 16), tokens)
     scale = jnp.asarray(HDIM**-0.5, BF)
-    query, upstream = qkv[own, col] * scale, a_all[own, col]
+    query, upstream = qkv[own, third(p, 0)] * scale, upstream_all[w, own, :]
     keys, values = qkv[:, third(p, 1)], qkv[:, third(p, 2)]
     mask = head_mask(tokens)
     zero = jnp.zeros_like(query)
     lanes = lax.broadcasted_iota(jnp.int32, (tokens, LANE), 1)
+    stats = cols[own, :]
     results = []
     for side in range(2):
         def pick(v):
             return jnp.where(mask, v, zero) if side == 0 else jnp.where(mask, zero, v)
-        total = jnp.sum(jnp.where(lanes == 2 * p + side, stats[...], 0.0), axis=-1, keepdims=True)
-        centre = jnp.sum(jnp.where(lanes == HEADS + 2 * p + side, stats[...], 0.0), axis=-1, keepdims=True)
+        total = jnp.sum(jnp.where(lanes == 2 * p + side, stats, 0.0), axis=-1, keepdims=True)
+        centre = jnp.sum(jnp.where(lanes == HEADS + 2 * p + side, stats, 0.0), axis=-1, keepdims=True)
         shares = jnp.exp(nt(pick(query), keys) - total)
         back = (shares * (nt(pick(upstream), values) - centre)).astype(BF) * scale
         results.append(nn(back, keys))
-    grad = jnp.where(mask, results[0], results[1])
-    pgrad[:, col] = grad.astype(BF)
-    v_qv[0:1, col] = jnp.sum(grad, axis=0, keepdims=True)
-
-
-def key_back(p, g, qkv, a_all, rows, pgrad, v_qv, tokens):
-    col = pl.ds(mo(p * LANE, LANE), LANE)
-    own = pl.ds(mo(g * tokens, 16), tokens)
+    store_grad(3 * w, own, jnp.where(mask, results[0], results[1]), pgh, csum)
+
+
+def store_grad(n, own, grad, pgh, csum):
+    col = pl.ds(mo(n * LANE, LANE), LANE)
+    pgh[own, col] = grad.astype(BF)
+    csum[0:1, col] = csum[0:1, col] + jnp.sum(grad, axis=0, keepdims=True)
+
+
+def key_back(w, p, j, qkv, upstream_all, rows, pgh, csum, tokens):
+    own = pl.ds(mo(j * tokens, 16), tokens)
     scale = jnp.asarray(HDIM**-0.5, BF)
     keys, values = qkv[own, third(p, 1)] * scale, qkv[own, third(p, 2)]
-    queries, upstream = qkv[:, col], a_all[:, col]
+    queries, upstream = qkv[:, third(p, 0)], upstream_all[w]
     mask = head_mask(tokens)
     zero = jnp.zeros_like(keys)
     ks, vs = [], []
@@ -237,10 +240,8 @@
         vs.append(nn(shares.astype(BF), upstream))
         back = (shares * (nt(pick(values), upstream) - centre)).astype(BF) * scale
         ks.append(nn(back, queries))
-    pgrad[:, pl.ds(mo(D + p * LANE, LANE), LANE)] = jnp.where(mask, ks[0], ks[1]).astype(BF)
-    grad = jnp.where(mask, vs[0], vs[1])
-    pgrad[:, pl.ds(mo(2 * D + p * LANE, LANE), LANE)] = grad.astype(BF)
-    v_qv[0:1, pl.ds(mo(D + p * LANE, LANE), LANE)] = jnp.sum(grad, axis=0, keepdims=True)
+    store_grad(3 * w + 1, own, jnp.where(mask, ks[0], ks[1]), pgh, csum)
+    store_grad(3 * w + 2, own, jnp.where(mask, vs[0], vs[1]), pgh, csum)
 
 
 def cell(ref, m, row, sub=None):
@@ -249,6 +250,9 @@
 
 
 ORDER = (3, 2, 1, 0)
+SUMS = (OUT, OUT, UP, DOWN)
+WHOLES = (UP, OUT, UP, DOWN)
+PAIR = 3 * LANE
 
 
 def layer_kernel(groups, highs, names, fr, ct, p_ref, oq, oo, ou, od, osm, out_frames, frames_grad, *scratch):
@@ -416,68 +420,120 @@
     def vcopy(i, owner):
         return remote(s.smb, s.sm.at[owner], s.ms.at[0], s.mr.at[0], rep, lax.rem(g + i, groups))
 
-    def place(r):
-        return s.a_all.at[pl.ds(mo(r * tokens, 16), tokens), :]
-
-    def scopy(d, step, r):
-        return remote(place(r), place(r), s.szs.at[d, step], s.szr.at[slot_of(d, step)], rep, toward(d))
+    def pair(owner, w):
+        return (3 * owner + 1) // 2 + w
+
+    def second(owner):
+        return lax.rem(owner, 2) == 0
+
+    def rows_at(r):
+        return pl.ds(mo(r * tokens, 16), tokens)
+
+    def scopy(i, w):
+        dest = lax.rem(g + i, groups)
+        return remote(s.agrad.at[:, third(pair(dest, w), 0)], s.a_h.at[w, rows_at(g), :], s.shs.at[w, i - 1], s.shr.at[w],
+                      rep, dest)
 
     def rcopy(i, owner):
         return remote(s.rows3.at[groups], s.rows3.at[owner], s.rs.at[0], s.rr.at[0], rep, lax.rem(g + i, groups))
 
     def share_start():
-        for d in range(2):
-            @pl.when(has_next(d))
+        for i in range(1, groups):
+            scopy(i, 0).start()
+
+            @pl.when(second(lax.rem(g + i, groups)))
             def _():
-                scopy(d, 0, g).start()
-        for i in range(1, groups):
+                scopy(i, 1).start()
             rcopy(i, g).start()
-
-    def share_step(step):
-        for d in range(2):
-            @pl.when(valid(d, step))
-            def _():
-                r = row_of(d, step)
-                scopy(d, step, r).wait_recv()
-                if step < last - 1:
-                    @pl.when(has_next(d))
-                    def _():
-                        scopy(d, step + 1, r).start()
-
-    def share_rows():
+        s.a_h[0, rows_at(g), :] = s.agrad[:, third(pair(g, 0), 0)]
+
+        @pl.when(second(g))
+        def _():
+            s.a_h[1, rows_at(g), :] = s.agrad[:, third(pair(g, 1), 0)]
+        s.csum[...] = jnp.zeros_like(s.csum)
+
+    def share_got():
+        arrived(s.a_h.at[0, pl.ds(0, last * tokens), :], s.shr.at[0])
+
+        @pl.when(second(g))
+        def _():
+            arrived(s.a_h.at[1, pl.ds(0, last * tokens), :], s.shr.at[1])
         arrived(s.rows3.at[pl.ds(0, last)], s.rr.at[0])
         for i in range(groups):
-            s.rows[:, i * tokens:(i + 1) * tokens] = s.rows3[i]
-        s.rows[:, pl.ds(mo(g * tokens, LANE), tokens)] = s.rows3[groups]
+            s.rows[0:2 * HEADS, i * tokens:(i + 1) * tokens] = s.rows3[i]
+        s.rows[0:2 * HEADS, pl.ds(mo(g * tokens, LANE), tokens)] = s.rows3[groups]
+        s.cols[...] = jnp.concatenate([s.rows[...], jnp.zeros((LANE - 2 * HEADS, groups * tokens), F32)], axis=0).T
 
     def share_sent():
-        for d in range(2):
-            @pl.when(has_next(d))
+        for i in range(1, groups):
+            scopy(i, 0).wait_send()
+
+            @pl.when(second(lax.rem(g + i, groups)))
             def _():
-                scopy(d, 0, g).wait_send()
-            for step in range(last - 1):
-                @pl.when(jnp.logical_and(valid(d, step), has_next(d)))
-                def _():
-                    scopy(d, step + 1, g).wait_send()
+                scopy(i, 1).wait_send()
         sent(s.rows3.at[pl.ds(0, last)], s.rs.at[0])
+
+    def bcopy_back(i, w, n):
+        dest = lax.rem(g + i, groups)
+        return remote(s.pgh.at[rows_at(dest), pl.ds((3 * w + n) * LANE, LANE)], s.pgrad.at[:, third(pair(g, w), n)],
+                      s.bks.at[w], s.bkr.at[0], rep, dest)
+
+    def each_pair(body):
+        body(0)
+
+        @pl.when(second(g))
+        def _():
+            body(1)
+
+    def return_queries():
+        def body(w):
+            for i in range(1, groups):
+                bcopy_back(i, w, 0).start()
+            s.pgrad[:, third(pair(g, w), 0)] = s.pgh[rows_at(g), 3 * w * LANE:(3 * w + 1) * LANE]
+        each_pair(body)
+
+    def return_keys(i):
+        def body(w):
+            for n in (1, 2):
+                if i:
+                    bcopy_back(i, w, n).start()
+                else:
+                    s.pgrad[:, third(pair(g, w), n)] = s.pgh[rows_at(g), (3 * w + n) * LANE:(3 * w + n + 1) * LANE]
+        each_pair(body)
+
+    def return_got():
+        @pl.when(second(g))
+        def _():
+            arrived(s.pgrad.at[:, pl.ds(0, 3 * D - 2 * PAIR)], s.bkr.at[0])
+
+        @pl.when(jnp.logical_not(second(g)))
+        def _():
+            arrived(s.pgrad.at[:, pl.ds(0, 3 * D - PAIR)], s.bkr.at[0])
+
+    def return_sent():
+        sent(s.pgh.at[pl.ds(0, last * tokens), pl.ds(0, PAIR)], s.bks.at[0])
+
+        @pl.when(second(g))
+        def _():
+            sent(s.pgh.at[pl.ds(0, last * tokens), pl.ds(0, PAIR)], s.bks.at[1])
 
     def row(i):
         return lax.rem(g + 1 + i, groups)
 
     def first(t, i):
-        m = MATS[t]
+        m = SUMS[t]
         at = pl.ds(mo(row(i) * m.block, 16), m.block)
         return remote(grads[t].at[at, pl.ds(mo((1 - h) * m.half, LANE), m.half)], s.buf1[t].at[at, :],
                       s.gone.at[t, i], s.c1r.at[t, i], core, g)
 
     def cell1(t, i, kk, sub=None):
-        return cell(s.buf1[t], MATS[t], row(i) * MATS[t].block + kk * MATS[t].quarter, sub)
+        return cell(s.buf1[t], SUMS[t], row(i) * SUMS[t].block + kk * SUMS[t].quarter, sub)
 
     def cell2(t, i, j, sub):
-        return cell(s.buf2[t], MATS[t], (row(i) * 2 + j) * MATS[t].quarter, sub)
+        return cell(s.buf2[t], SUMS[t], (row(i) * 2 + j) * SUMS[t].quarter, sub)
 
     def cell3(t, i, sub=None):
-        return cell(s.buf3[t], MATS[t], row(i) * MATS[t].quarter, sub)
+        return cell(s.buf3[t], SUMS[t], row(i) * SUMS[t].quarter, sub)
 
     def a1(t, i, j, kk):
         return remote(cell1(t, i, kk, 0), cell2(t, i, j, 0), s.gone.at[t, i], s.ab1r.at[t, i], xn, g)
@@ -501,8 +557,11 @@
     def z3(t):
         return remote(cell3(t, 1), s.zbuf[t].at[2], s.gone.at[t, 1], s.z2r.at[t, 2], rep, flip(g, 2))
 
+    def z4(i):
+        return remote(cell3(0, i), s.fin[0].at[0, :, pl.ds(mo(g * PAIR, LANE), PAIR)], s.gone.at[0, i], s.zqr.at[0], rep, row(i))
+
     def r1(t, i):
-        m = MATS[t]
+        m = SUMS[t]
         first(t, i).wait_recv()
         at = pl.ds(mo(row(i) * m.block, 16), m.block)
         mine = grads[t].at[at, pl.ds(mo(h * m.half, LANE), m.half)]
@@ -512,7 +571,7 @@
             b1(t, i, j, 2 * (1 - y) + j).start()
 
     def r2(t, i):
-        m = MATS[t]
+        m = SUMS[t]
         arrived(s.buf2[t].at[pl.ds(mo(row(i) * 2 * m.quarter, 16), 2 * m.quarter), :], s.ab1r.at[t, i])
         for j in range(2):
             add_rows(cell2(t, i, j, 0), cell1(t, i, 2 * j + x, 0), cell2(t, i, j, 0), m.sub[0][1])
@@ -522,20 +581,25 @@
         b2(t, i, 1 - x).start()
 
     def r3(t, i):
-        m = MATS[t]
+        m = SUMS[t]
         arrived(cell3(t, i), s.ab2r.at[t, i])
         add_rows(cell3(t, i, 0), cell2(t, i, y, 0), cell3(t, i, 0), m.sub[0][1])
         add_rows(cell3(t, i, 1), cell2(t, i, x, 1), cell3(t, i, 1), m.sub[1][1])
-        if i % 2 == 0:
+        if t == 0:
+            if i < last:
+                z4(i).start()
+            else:
+                s.fin[0][0, :, pl.ds(mo(g * PAIR, LANE), PAIR)] = cell3(0, last)[...]
+        elif i % 2 == 0:
             z2(t, i).start()
 
     def r3b(t):
         z2_got(t, 0)
-        add_rows(cell3(t, 1), cell3(t, 1), s.zbuf[t].at[0], MATS[t].quarter)
+        add_rows(cell3(t, 1), cell3(t, 1), s.zbuf[t].at[0], SUMS[t].quarter)
         z3(t).start()
 
     def fpart(t, kk, hh, sub=None):
-        return part(outs[t], MATS[t], 0, kk, hh, sub)
+        return part(outs[t], WHOLES[t], 0, kk, hh, sub)
 
     def keep(t):
         return pltpu.make_async_copy(s.fin[t].at[0], fpart(t, k, h), s.os.at[t])
@@ -557,20 +621,24 @@
         return remote(reg, reg, s.osent.at[t], s.oar.at[t], (yn, xn)[sub], g)
 
     def cross(t, hh):
-        reg = slab(outs[t], MATS[t], 0, hh)
+        reg = slab(outs[t], WHOLES[t], 0, hh)
         return remote(reg, reg, s.osent.at[t], s.ocr.at[t], core, g)
 
     def r4(t):
-        m = MATS[t]
-        z2_got(t, 1)
-        z3(t).wait_recv()
+        m = WHOLES[t]
+        if t == 0:
+            arrived(s.fin[0].at[0, :, pl.ds(0, last * PAIR)], s.zqr.at[0])
+        else:
+            z2_got(t, 1)
+            z3(t).wait_recv()
         mine = cell3(t, last)
 
         def body(n):
             at = pl.ds(mo(n * 16, 16), 16)
             total = mine[at, :].astype(F32) + s.zbuf[t][1, at, :].astype(F32) + s.zbuf[t][2, at, :].astype(F32)
             s.fin[t][0, at, :] = total.astype(BF)
-        loop(m.quarter // 16, body)
+        if t:
+            loop(m.quarter // 16, body)
         for b in range(highs):
             cp = remote(s.fin[t].at[0], s.fin[t].at[1 + b], s.fxs.at[t, b], s.fxr.at[t, b], flip(rep, 8 << b), g)
             cp.start()
@@ -591,11 +659,12 @@
         keep(t).wait()
         cross(t, h).start()
 
-    partners = [(core, g), (xn, g), (yn, g)] + [(flip(rep, 8 << b), g) for b in range(highs)]
+    partners = []
     bit = 1
     while bit < groups:
         partners.append((rep, flip(g, bit)))
         bit *= 2
+    partners += [(core, g), (xn, g), (yn, g)] + [(flip(rep, 8 << b), g) for b in range(highs)]
 
     def smcopy(j):
         return remote(s.smacc.at[j], s.smin.at[j], s.sms.at[j], s.smr.at[j], *partners[j])
@@ -615,14 +684,14 @@
 
     def chunks_sent():
         for t in ORDER:
-            m = MATS[t]
+            m = SUMS[t]
             for i in range(groups):
                 sent(grads[t].at[pl.ds(0, (8 if i < last else 7) * m.quarter), pl.ds(0, m.half)], s.gone.at[t, i])
 
     def outs_sent():
         sent(s.sm.at[pl.ds(0, last)], s.ms.at[0])
         for t in ORDER:
-            m = MATS[t]
+            m = WHOLES[t]
             sent(grads[t].at[pl.ds(0, 7 * m.quarter), pl.ds(0, m.half)], s.osent.at[t])
         for j in range(len(partners)):
             smcopy(j).wait_send()
@@ -641,9 +710,7 @@
             c = block(n)
             s.middle[:, c] = nn(s.attended[...], s.wo[:, c]) + s.obias[0:1, c] + fr[:, c].astype(F32)
         loop(D // 256, body)
-        value, inverse = normalize(s.middle[...])
-        s.normal[...] = value
-        s.inverse[...] = jnp.broadcast_to(inverse, (tokens, LANE))
+        value, _ = normalize(s.middle[...])
         s.normed[...] = (value * s.gain2[...] + s.shift2[...]).astype(BF)
 
     def hidden(i):
@@ -671,25 +738,25 @@
         loop(D // 256, body)
 
     def back_norm():
-        upstream, normal = s.wide[...], s.normal[...]
+        upstream = s.wide[...]
+        normal, inverse = normalize(s.middle[...])
         s.v_gain2[...] = jnp.sum(upstream * normal, axis=0, keepdims=True)
         s.v_shift2[...] = jnp.sum(upstream, axis=0, keepdims=True)
-        total = ct[...].astype(F32) + norm_back(upstream, normal, s.inverse[:, 0:1], s.gain2[...])
+        total = ct[...].astype(F32) + norm_back(upstream, normal, inverse, s.gain2[...])
         s.mgrad[...] = total
         s.half[...] = total.astype(BF)
         s.v_out[...] = jnp.sum(total, axis=0, keepdims=True)
         s.v_down[...] = jnp.sum(ct[...].astype(F32), axis=0, keepdims=True)
 
         def body(n):
-            s.a_all[own, block(n)] = nt(s.half[...], s.wo[block(n), :]).astype(BF)
-        own = pl.ds(mo(g * tokens, 16), tokens)
+            s.agrad[:, block(n)] = nt(s.half[...], s.wo[block(n), :]).astype(BF)
         loop(D // 256, body)
         lanes = lax.broadcasted_iota(jnp.int32, (tokens, LANE), 1)
         mask = head_mask(tokens)
         stats = s.stats[...]
         for p in range(HEADS // 2):
             c = slice(p * LANE, (p + 1) * LANE)
-            product = s.a_all[own, c].astype(F32) * s.attended[:, c].astype(F32)
+            product = s.agrad[:, c].astype(F32) * s.attended[:, c].astype(F32)
             for side in range(2):
                 mine = jnp.where(mask if side == 0 else jnp.logical_not(mask), product, 0.0)
                 stats = jnp.where(lanes == HEADS + 2 * p + side, jnp.sum(mine, axis=-1, keepdims=True), stats)
@@ -717,30 +784,62 @@
         for i in (0, 2, 1, 3):
             first(t, i).start()
 
-    def queries(p):
-        loop(2, lambda i: query_back(p + i, g, s.qkv, s.a_all, s.stats, s.pgrad, s.v_qv, tokens))
-
-    def keys(p):
-        loop(2, lambda i: key_back(p + i, g, s.qkv, s.a_all, s.rows, s.pgrad, s.v_qv, tokens))
-
-    def to_inputs():
-        normal, _ = normalize(fr[...].astype(F32))
-        s.normed[...] = (normal * s.gain1[...] + s.shift1[...]).astype(BF)
-        turn(s.normed, s.turned)
+    pairs_here = 2 - lax.rem(g, 2)
+
+    def queries(j):
+        loop(pairs_here, lambda w: query_back(w, pair(g, w), j, s.qkv, s.a_h, s.cols, s.pgh, s.csum, tokens))
+
+    def keys(i):
+        j = lax.rem(g + i, groups)
+        loop(pairs_here, lambda w: key_back(w, pair(g, w), j, s.qkv, s.a_h, s.rows, s.pgh, s.csum, tokens))
+
+    def turn_all():
+        def body(j):
+            normal, _ = normalize(s.fa[rows_at(j), :].astype(F32))
+            s.turned_all[:, pl.ds(mo(j * tokens, LANE), tokens)] = normal.astype(BF).T
+        loop(groups, body)
+
+    def weight_pairs():
+        s.acc[...] = jnp.zeros_like(s.acc)
+
+        def body(w):
+            product = nn(s.turned_all[...], s.pgh[:, pl.ds(mo(w * PAIR, LANE), PAIR)])
+            sums = s.csum[0:1, pl.ds(mo(w * PAIR, LANE), PAIR)]
+            s.wu[:, pl.ds(mo(w * PAIR, LANE), PAIR)] = (product * s.columns[:, 0:1] + s.columns[:, 1:2] * sums).astype(BF)
+            for n in range(3):
+                weights = s.wq[:, third(pair(g, w), n)].astype(F32)
+                c = slice(n * LANE, (n + 1) * LANE)
+                s.acc[0] = s.acc[0] + weights * product[:, c]
+                s.acc[1] = s.acc[1] + weights * sums[:, c]
+        loop(pairs_here, body)
+
+        @pl.when(jnp.logical_not(second(g)))
+        def _():
+            s.wu[:, PAIR:2 * PAIR] = jnp.zeros((D, PAIR), BF)
+        for i in (0, 2, 1, 3):
+            first(0, i).start()
+
+    def send_small():
+        s.v_gain1[...] = jnp.sum(s.acc[0].T, axis=0, keepdims=True)
+        s.v_shift1[...] = jnp.sum(s.acc[1].T, axis=0, keepdims=True)
+        s.v_qv[...] = jnp.zeros_like(s.v_qv)
+
+        def body(w):
+            p = pair(g, w)
+            s.v_qv[0:1, third(p, 0)] = s.csum[0:1, pl.ds(mo(w * PAIR, LANE), LANE)]
+            s.v_qv[0:1, third(p, 1)] = s.csum[0:1, pl.ds(mo(w * PAIR + 2 * LANE, LANE), LANE)]
+        loop(pairs_here, body)
+        fill_image(s.smacc.at[0], range(SROWS), (
+            (GAIN_ONE, s.v_gain1), (SHIFT_ONE, s.v_shift1), (QV_BIAS, s.v_qv), (OUT_BIAS, s.v_out), (GAIN_TWO, s.v_gain2),
+            (SHIFT_TWO, s.v_shift2), (UP_BIAS, s.v_up), (DOWN_BIAS, s.v_down)))
+        small(0)
 
     def input_grad():
         def body(n):
             s.wide[:, block(n)] = nt(s.pgrad[...], s.wq[block(n), :])
         loop(D // 256, body)
         normal, inverse = normalize(fr[...].astype(F32))
-        upstream = s.wide[...]
-        s.v_gain1[...] = jnp.sum(upstream * normal, axis=0, keepdims=True)
-        s.v_shift1[...] = jnp.sum(upstream, axis=0, keepdims=True)
-        frames_grad[...] = (s.mgrad[...] + norm_back(upstream, normal, inverse, s.gain1[...])).astype(BF)
-        fill_image(s.smacc.at[0], range(SROWS), (
-            (GAIN_ONE, s.v_gain1), (SHIFT_ONE, s.v_shift1), (QV_BIAS, s.v_qv), (OUT_BIAS, s.v_out), (GAIN_TWO, s.v_gain2),
-            (SHIFT_TWO, s.v_shift2), (UP_BIAS, s.v_up), (DOWN_BIAS, s.v_down)))
-        small(0)
+        frames_grad[...] = (s.mgrad[...] + norm_back(s.wide[...], normal, inverse, s.gain1[...])).astype(BF)
 
     barrier, peers = greet(rep, g, groups)
     peers += [(flip(rep, 8 << b), g) for b in range(highs)]
@@ -789,6 +888,8 @@
     for spot, ref in ((GAIN_ONE, s.gain1), (SHIFT_ONE, s.shift1), (QV_BIAS, s.qvbias), (GAIN_TWO, s.gain2), (SHIFT_TWO, s.shift2),
                       (OUT_BIAS, s.obias), (UP_BIAS, s.ubias), (DOWN_BIAS, s.dbias)):
         assemble(s.sm, spot, ref)
+    lower = lax.broadcasted_iota(jnp.int32, (LANE, D), 0) == 0
+    s.columns[...] = jnp.where(lower, s.gain1[...], s.shift1[...]).T
     s.bias3[...] = jnp.zeros_like(s.bias3)
     s.bias3[0:1, 0:D] = s.qvbias[0:1, 0:D]
     s.bias3[0:1, 2 * D:3 * D] = s.qvbias[0:1, D:2 * D]
@@ -847,6 +948,7 @@
         if t == 1:
             both(3, t, step)
     to_middle()
+    turn_all()
     for t, step in rest:
         if t > 1:
             both(3, t, step)
@@ -865,91 +967,86 @@
     r1(3, 2)
     weight(3, 3, s.act, ct)
     r1(3, 1)
-    turn(s.normed, s.turned2)
+    turn(s.normed, s.turned)
     r1(3, 3)
     r2(3, 2)
-    weight_all(2, s.turned2, s.pre)
+    weight_all(2, s.turned, s.pre)
     r2(3, 1)
     r1(2, 0)
-    to_output()
-    share_step(0)
+    share_got()
     r1(2, 2)
+    turn(s.attended, s.turned)
+    weight_all(1, s.turned, s.half)
     r2(3, 3)
-    turn(s.attended, s.turned2)
-    weight_all(1, s.turned2, s.half)
-    gather_sent()
+    queries(0)
+    r3(3, 0)
+    r3(3, 2)
+    queries(1)
     r2(2, 0)
     r1(2, 1)
-    queries(0)
-    share_step(1)
+    queries(2)
+    gather_sent()
+    r3(3, 1)
+    r3(3, 3)
+    queries(3)
     r2(2, 2)
     r1(2, 3)
-    queries(2)
-    queries(4)
+    keys(1)
+    r3b(3)
     r2(2, 1)
-    r1(1, 0)
-    r1(1, 2)
-    share_step(2)
-    share_rows()
-    r3(3, 0)
-    r3(3, 2)
-    keys(0)
+    for i in (0, 2, 1, 3):
+        r1(1, i)
+    keys(2)
+    r3(2, 0)
+    r3(2, 2)
     r2(2, 3)
-    r1(1, 1)
-    r1(1, 3)
-    r3(3, 1)
-    r3(3, 3)
+    keys(3)
     r2(1, 0)
     r2(1, 2)
-    to_inputs()
-    keys(2)
+    keys(0)
+    r3(2, 1)
+    r3(2, 3)
+    r4(3)
+    r3b(2)
+    return_queries()
+    weight_pairs()
     r2(1, 1)
     r2(1, 3)
-    keys(4)
-    r3b(3)
-    r3(2, 0)
-    r3(2, 2)
-    weight_all(0, s.turned, s.pgrad)
-    r3(2, 1)
-    r3(2, 3)
-    input_grad()
-    r1(0, 0)
-    r1(0, 2)
-    r4(3)
-    r2(0, 0)
-    r2(0, 2)
-    r1(0, 1)
-    r1(0, 3)
+    send_small()
+    r5(3)
+    for i in (0, 2, 1, 3):
+        r1(0, i)
     r3(1, 0)
     r3(1, 2)
-    r3b(2)
-    r3(0, 0)
-    r3(0, 2)
-    r5(3)
-    r2(0, 1)
-    small(1)
+    for i in (0, 2, 1, 3):
+        r2(0, i)
+    r6(3)
     r3(1, 1)
     r3(1, 3)
-    r2(0, 3)
     r4(2)
-    r6(3)
+    for i in (0, 2, 1, 3):
+        r3(0, i)
+    small(1)
     r3b(1)
-    r3(0, 1)
-    r3(0, 3)
-    r3b(0)
+    for i in (1, 2, 3, 0):
+        return_keys(i)
+    to_output()
     r5(2)
+    small(2)
+    r4(0)
+    r6(2)
+    small(3)
     r4(1)
-    small(2)
-    r6(2)
-    r4(0)
+    small(4)
+    r5(0)
     r5(1)
-    small(3)
-    r5(0)
-    small(4)
-    r6(1)
-    r6(0)
     for j in range(5, len(partners) + 1):
         small(j)
+    r6(0)
+    r6(1)
+    return_got()
+    input_grad()
+    return_sent()
     crossed()
     share_sent()
     chunks_sent()
@@ -972,15 +1069,16 @@
 
     scratch = {name: bf(m.block * groups, m.cols) for name, m in zip(("wq", "wo", "wu", "wd"), MATS)}
     scratch.update(go=bf(D, D), gu=bf(D, FF), gd=bf(FF, D))
-    scratch.update(buf1=[bf(m.block * groups, m.half) for m in MATS], buf2=[bf(m.quarter * groups * 2, m.half) for m in MATS],
-                   buf3=[bf(m.quarter * groups, m.half) for m in MATS], zbuf=[bf(groups - 1, m.quarter, m.half) for m in MATS],
-                   fin=[bf(highs + 1, m.quarter, m.half) for m in MATS])
-    scratch.update(fa=bf(clip, D), qkv=bf(clip, 3 * D), a_all=bf(clip, D))
+    scratch.update(buf1=[bf(m.block * groups, m.half) for m in SUMS], buf2=[bf(m.quarter * groups * 2, m.half) for m in SUMS],
+                   buf3=[bf(m.quarter * groups, m.half) for m in SUMS], zbuf=[bf(groups - 1 if t else 1, m.quarter, m.half) for t, m in enumerate(SUMS)],
+                   fin=[bf(highs + 1, m.quarter, m.half) for m in WHOLES])
+    scratch.update(fa=bf(clip, D), qkv=bf(clip, 3 * D), a_h=bf(2, clip, LANE), agrad=bf(tokens, D), pgh=bf(clip, 2 * PAIR), turned_all=bf(D, clip))
     scratch.update(attended=bf(tokens, D), normed=bf(tokens, D), half=bf(tokens, D),
-                   act=bf(tokens, FF), pre=bf(tokens, FF), pgrad=bf(tokens, 3 * D), turned=bf(D, tokens), turned2=bf(D, tokens))
-    scratch.update(middle=wide(tokens, D), normal=wide(tokens, D), mgrad=wide(tokens, D), wide=wide(tokens, D),
-                   inverse=wide(tokens, LANE), stats=wide(tokens, LANE))
-    scratch.update(rows3=wide(groups + 1, 2 * HEADS, tokens), rows=wide(2 * HEADS, clip))
+                   act=bf(tokens, FF), pre=bf(tokens, FF), pgrad=bf(tokens, 3 * D), turned=bf(D, tokens))
+    scratch.update(middle=wide(tokens, D), mgrad=wide(tokens, D), wide=wide(tokens, D),
+                   stats=wide(tokens, LANE))
+    scratch.update(rows3=wide(groups + 1, 2 * HEADS, tokens), rows=wide(2 * HEADS, clip), cols=wide(clip, LANE), csum=wide(1, 2 * PAIR),
+                   columns=wide(D, LANE), acc=wide(2, D, LANE))
     scratch.update({name: wide(1, D) for name in ("gain1", "shift1", "gain2", "shift2", "obias", "dbias", "v_gain1", "v_shift1",
                                                   "v_gain2", "v_shift2", "v_out", "v_down")})
     scratch.update(qvbias=wide(1, 2 * D), bias3=wide(1, 3 * D), v_qv=wide(1, 2 * D), ubias=wide(1, FF), v_up=wide(1, FF))
@@ -991,7 +1089,7 @@
     scratch.update(lsem=dma((3,)), ssem=dma((2,)), zs=dma((4,)), zfs=dma((2, groups - 1)), zr=dma((5, groups - 1)))
     scratch.update({name: dma((4, groups - 1)) for name in ("gs", "xr", "yr", "fr", "cr", "z2r")})
     scratch.update({name: dma((1,)) for name in ("ms", "mr", "rs", "rr")})
-    scratch.update(szs=dma((2, groups - 1)), szr=dma((groups - 1,)))
+    scratch.update(shs=dma((2, groups - 1)), shr=dma((2,)), bks=dma((2,)), bkr=dma((1,)), zqr=dma((1,)))
     scratch.update({name: dma((4, groups)) for name in ("gone", "c1r", "ab1r", "ab2r")})
     if highs:
         scratch.update({name: dma((4, highs)) for name in ("fxs", "fxr")})
@@ -1008,7 +1106,7 @@
 
     return pl.pallas_call(
         body,
-        out_shape=[sds((m.block, m.cols), BF) for m in MATS] + [sds((SROWS, LANE), F32), sds((tokens, D), BF), sds((tokens, D), BF)],
+        out_shape=[sds((m.block, m.cols), BF) for m in WHOLES] + [sds((SROWS, LANE), F32), sds((tokens, D), BF), sds((tokens, D), BF)],
         in_specs=[vmem, vmem, hbm],
         out_specs=[hbm] * 4 + [vmem] * 3,
         scratch_shapes=flat,
@@ -1032,7 +1130,9 @@
     def body(i):
         base = m.row0 + i * (48 * m.tiles)
         for c in range(m.tiles):
-            tile = block[pl.ds(mo(i * 48, 16), 48), c * LANE:(c + 1) * LANE].astype(F32)
+            at = (c % (m.tiles // 3)) if m is QKV else 0
+            at = (at % 3 == 1) * 12 + (0, 0, 1, 2, 2, 3)[at] * 3 + c // (m.tiles // 3) if m is QKV else c
+            tile = block[pl.ds(mo(i * 48, 16), 48), at * LANE:(at + 1) * LANE].astype(F32)
             if m.shifted:
                 tile = pltpu.roll(tile, 64, 1)
                 late[pl.ds(base + c + 1, 48, stride=m.tiles), :] = tile

time: 204 us -> 199 us (0.975)
  Pallas kernels: 201 us -> 198 us
    pallas_call x1, Pallas kernels: 177 us -> 174 us  [layer(): pl.pallas_call(body, out_shape=[sds((m.block, m.cols), BF) for m in WHOLE...]
where the time goes in v1:
time: 199 us
  Pallas kernels  198 us (99%)
    pallas_call x1, Pallas kernels, layer(): pl.pallas_call(body, out_shape=[sds((m.block, m.cols), BF) for m in WHOLE...  174 us
    pallas_call x1, Pallas kernels, adam(): pl.pallas_call(functools.partial(adam_kernel, 1.0 / reps), out_shape=[jax...  24.1 us

profile of v1, /device:TPU:28, one launch (start us, length us, event | category | flops | bytes accessed | tf_op | source)
XLA Modules:
  0.0 198.6 jit_solution(11480851949236187159)
XLA Ops:
  0.6 173.7 %layer.1 = (bf16[192,3072]{1,0:T(8,128)(2,1)}, bf16[192,768]{1,0:T(8,128)(2,1)}, bf16[192,3072]{1,0:T(8,128)(2,1)}, bf16[768,768]{1,0:T(8,128)(2,1)}, f32[24,128...) custom-call(bf16[256,768]{1,0:T(8,128)(2,1)} %refs_0_.1, bf16[256,768]{1,0:T(8,128)(2,1)} %refs_1_.1, ...), custom_call_target="tpu_custom_call" | custom-call | tf_op jit(solution)/shard_map/layer/pallas_call | solution.py:1107
  174.3 24.1 %adam.1 = (f32[1,1771776]{1,0:T(1,128)}, f32[1,1771776]{1,0:T(1,128)}, f32[1,1771776]{1,0:T(1,128)}, f32[1,1771776]{1,0:T(1,128)}, bf16[256,768]{1,0:T(8,128)(2,1)}, /*index=5*/bf16[256,768]{1,0:T(8,128)(2,1)}) custom-call(bf16[192,3072]{1,0:T(8,128)(2,1)} %get-tuple-element.19.gq, bf16[192,768]{1,0:T(8,128)(2,1)} %get-tuple-element.20.go, ...), custom_call_target="tpu_custom_call" | custom-call | tf_op jit(solution)/shard_map/adam/pallas_call | solution.py:1237

commit v2 on v1

--- a/solution.py
+++ b/solution.py
@@ -167,10 +167,11 @@
     return pl.ds(mo(n * D + p * LANE, LANE), LANE)
 
 
-def project_block(j, fa, gain, shift, bias, wq, qkv, normed, tokens):
+def project_block(j, fa, gain, shift, bias, wq, qkv, normed, turned, tokens):
     at = pl.ds(mo(j * tokens, 16), tokens)
     normal, _ = normalize(fa[at, :].astype(F32))
     normed[...] = (normal * gain[...] + shift[...]).astype(BF)
+    turned[:, pl.ds(mo(j * tokens, LANE), tokens)] = normal.astype(BF).T
 
     def body(n):
         col = pl.ds(mo(n * 256, 256), 256)
@@ -697,7 +698,7 @@
             smcopy(j).wait_send()
 
     def project(j):
-        project_block(j, s.fa, s.gain1, s.shift1, s.bias3, s.wq, s.qkv, s.normed, tokens)
+        project_block(j, s.fa, s.gain1, s.shift1, s.bias3, s.wq, s.qkv, s.normed, s.turned_all, tokens)
 
     def attention(p):
         loop(2, lambda i: attend_pair(p + i, g, s.qkv, s.attended, s.stats, tokens))
@@ -792,12 +793,6 @@
     def keys(i):
         j = lax.rem(g + i, groups)
         loop(pairs_here, lambda w: key_back(w, pair(g, w), j, s.qkv, s.a_h, s.rows, s.pgh, s.csum, tokens))
-
-    def turn_all():
-        def body(j):
-            normal, _ = normalize(s.fa[rows_at(j), :].astype(F32))
-            s.turned_all[:, pl.ds(mo(j * tokens, LANE), tokens)] = normal.astype(BF).T
-        loop(groups, body)
 
     def weight_pairs():
         s.acc[...] = jnp.zeros_like(s.acc)
@@ -948,7 +943,6 @@
         if t == 1:
             both(3, t, step)
     to_middle()
-    turn_all()
     for t, step in rest:
         if t > 1:
             both(3, t, step)
@@ -1013,14 +1007,13 @@
     r2(1, 1)
     r2(1, 3)
     send_small()
-    r5(3)
     for i in (0, 2, 1, 3):
         r1(0, i)
+    r5(3)
     r3(1, 0)
     r3(1, 2)
     for i in (0, 2, 1, 3):
         r2(0, i)
-    r6(3)
     r3(1, 1)
     r3(1, 3)
     r4(2)
@@ -1031,21 +1024,22 @@
     for i in (1, 2, 3, 0):
         return_keys(i)
     to_output()
+    r6(3)
     r5(2)
     small(2)
     r4(0)
+    r4(1)
+    small(3)
+    r5(0)
     r6(2)
-    small(3)
-    r4(1)
+    r5(1)
     small(4)
-    r5(0)
-    r5(1)
-    for j in range(5, len(partners) + 1):
-        small(j)
     r6(0)
     r6(1)
     return_got()
     input_grad()
+    for j in range(5, len(partners) + 1):
+        small(j)
     return_sent()
     crossed()
     share_sent()
@@ -1164,6 +1158,8 @@
     loads[1].start()
     fetch(1)
     loads[2].start()
+    fetch(2)
+    loads[3].start()
 
     def update(c):
         for cp in ins[c]:
@@ -1186,7 +1182,7 @@
             current = pb[lanes].astype(F32)
             nb[lanes] = current - LEARN_RATE * (first_hat / (jnp.sqrt(second_hat) + ADAM_EPS) + DECAY * current)
         loop(-(-min(ROWS, FROWS - c * ROWS) // SUB), body)
-        fetch(c + 2)
+        fetch(c + 3)
         for cp in puts[c]:
             cp.start()
 
@@ -1204,10 +1200,9 @@
     flat[4618:4619, 0:64] = sm[10:11, 0:64]
     flat[9226:9227, 64:128] = sm[11:12, 64:128]
     update(2)
-    loads[3].start()
+    update(3)
     for cp in takes:
         cp.start()
-    update(3)
     update(4)
     loads[3].wait()
     flatten(DOWN, bd, flat, late)

time: 199 us -> 192 us (0.965)
  Pallas kernels: 198 us -> 191 us
    pallas_call x1, Pallas kernels: 24.1 us -> 20.4 us  [adam(): pl.pallas_call(functools.partial(adam_kernel, 1.0 / reps), out_shape=[jax...]
    pallas_call x1, Pallas kernels: 174 us -> 171 us  [layer(): pl.pallas_call(body, out_shape=[sds((m.block, m.cols), BF) for m in WHOLE...]
where the time goes in v2:
time: 192 us
  Pallas kernels  191 us (99%)
    pallas_call x1, Pallas kernels, layer(): pl.pallas_call(body, out_shape=[sds((m.block, m.cols), BF) for m in WHOLE...  171 us
    pallas_call x1, Pallas kernels, adam(): pl.pallas_call(functools.partial(adam_kernel, 1.0 / reps), out_shape=[jax...  20.4 us

profile of v2, /device:TPU:28, one launch (start us, length us, event | category | flops | bytes accessed | tf_op | source)
XLA Modules:
  0.0 191.8 jit_solution(17194649776138721113)
XLA Ops:
  0.6 170.5 %layer.1 = (bf16[192,3072]{1,0:T(8,128)(2,1)}, bf16[192,768]{1,0:T(8,128)(2,1)}, bf16[192,3072]{1,0:T(8,128)(2,1)}, bf16[768,768]{1,0:T(8,128)(2,1)}, f32[24,128...) custom-call(bf16[256,768]{1,0:T(8,128)(2,1)} %refs_0_.1, bf16[256,768]{1,0:T(8,128)(2,1)} %refs_1_.1, ...), custom_call_target="tpu_custom_call" | custom-call | tf_op jit(solution)/shard_map/layer/pallas_call | solution.py:1101
  171.2 20.4 %adam.1 = (f32[1,1771776]{1,0:T(1,128)}, f32[1,1771776]{1,0:T(1,128)}, f32[1,1771776]{1,0:T(1,128)}, f32[1,1771776]{1,0:T(1,128)}, bf16[256,768]{1,0:T(8,128)(2,1)}, /*index=5*/bf16[256,768]{1,0:T(8,128)(2,1)}) custom-call(bf16[192,3072]{1,0:T(8,128)(2,1)} %get-tuple-element.19.gq, bf16[192,768]{1,0:T(8,128)(2,1)} %get-tuple-element.20.go, ...), custom_call_target="tpu_custom_call" | custom-call | tf_op jit(solution)/shard_map/adam/pallas_call | solution.py:1232
